TPU v7x, 32 devices: a whole 2x2x4 slice. The times are simulated.
32 devices in a mesh: grp: 4 (over y, core), vocab: 8 (over z, x).
Axes of the slice: x: 2, y: 2, z: 4, core: 2. Of those that a mesh axis runs over, the one named last changes fastest.
Arguments:
- hidden: bfloat16 [2048, 3584], P(('grp', 'vocab')), may hold values from -6 to 6
- embedding: bfloat16 [32768, 3584], P(('vocab', 'grp')), may hold values from -0.75 to 0.75
- targets: int32 [2048], P(('grp', 'vocab')), may hold values from 0 to 32767
- segments: int32 [2048], P(('grp', 'vocab')), may hold values from 0 to 15, never falling along the last dimension, each value on 1 to 256 neighbouring positions
Outputs:
- token_loss: float32 [2048], P(('grp', 'vocab'))
- doc_zloss: float32 [16], replicated
Inputs may be any that keep to these rules, and one draw needn't show every extreme that they name: `segments`: segment ids never fall along the tokens; each document has 1 to 256 tokens.
All inputs are finite; a program needn't handle non-finite values.
Results may differ from a plain program's by a relative error of at most 0.0003.
Values may be sent and summed in bfloat16 or wider, within the bound.
A program may use at most 128 MiB of HBM per device.

v0:
```python
import jax
import jax.numpy as jnp
from jax import lax
from jax.sharding import PartitionSpec as P

DOC_GRP = 4


soft_cap = 30.0
zloss_coef = 0.0001


def partial_stats(rows_hidden, rows_targets, table, idents):
    logits = lax.dot_general(
        rows_hidden, table, (((1,), (1,)), ((), ())), preferred_element_type=jnp.float32
    )
    capped = soft_cap * jnp.tanh(logits / soft_cap)
    sumexp = jnp.sum(jnp.exp(capped - soft_cap), axis=1)
    hit = idents[None, :] == rows_targets[:, None]
    picked = jnp.sum(jnp.where(hit, capped, jnp.zeros_like(capped)), axis=1)
    return (sumexp, picked)


def body(hidden, embedding, targets, segments):
    shard_rows = embedding.shape[0]
    vocab_start = (
        lax.axis_index("vocab") * lax.axis_size("grp") + lax.axis_index("grp")
    ) * shard_rows
    idents = vocab_start + lax.iota(jnp.int32, shard_rows)
    sumexp, picked = partial_stats(
        lax.all_gather(hidden, ("grp", "vocab"), axis=0, tiled=True),
        lax.all_gather(targets, ("grp", "vocab"), axis=0, tiled=True),
        embedding,
        idents,
    )
    own_total, own_picked = (
        lax.psum_scatter(sumexp, ("grp", "vocab"), scatter_dimension=0, tiled=True),
        lax.psum_scatter(picked, ("grp", "vocab"), scatter_dimension=0, tiled=True),
    )
    lse = soft_cap + jnp.log(own_total)
    zterm = zloss_coef * lse * lse
    token_loss = lse - own_picked + zterm
    documents = DOC_GRP * lax.axis_size("grp")
    onehot = (segments[:, None] == lax.iota(jnp.int32, documents)[None, :]).astype(jnp.float32)
    local_sums = jnp.dot(zterm, onehot, precision=lax.Precision.HIGHEST)
    doc_zloss = lax.psum(local_sums, ("grp", "vocab"))
    return (token_loss, doc_zloss)


def solution(mesh):
    return jax.shard_map(
        body,
        mesh=mesh,
        in_specs=(
            P(("grp", "vocab"), None),
            P(("vocab", "grp"), None),
            P(("grp", "vocab")),
            P(("grp", "vocab")),
        ),
        out_specs=(P(("grp", "vocab")), P()),
        check_vma=False,
    )
```

profile of v0, /device:TPU:0, one launch (start us, length us, event | category | flops | bytes accessed | tf_op | source)
XLA Modules:
  0.0 228.3 jit_solution(13362004366622051790)
XLA Ops:
  7.2 0.0 all-gather.2.cloned.1.call-start
  7.2 0.7 all-gather.2.cloned.1.call-update
  7.9 0.9 dynamic-update-slice
  8.8 43.3 %all-reduce = s32[2048]{0:T(1024)S(1)} all-reduce(s32[2048]{0:T(1024)S(1)} %dynamic-update-slice), channel_id=1, replica_groups=mesh['grp'=4,'vocab'=8] {'grp','vocab'}, use_global_device_ids=true, to_apply=%add | all-reduce | flops 2048 | bytes 16384
  52.1 0.0 copy-start
  52.1 67.3 %all-gather.2.cloned.1.call-done = bf16[2048,3584]{1,0:T(8,128)(2,1)} async-done(((bf16[64,3584]{1,0:T(8,128)(2,1)}), bf16[2048,3584]{1,0:T(8,128)(2,1)}) %all-gather.2.cloned.1.call-update) | async-done | bytes 14680080 | tf_op jit(solution)/shard_map/all_gather | solution.py:31
  119.4 22.0 %exponential_reduce_fusion = (f32[2048]{0:T(1024)S(1)}, f32[2048]{0:T(1024)S(1)}) fusion(s32[2048]{0:T(1024)S(1)} %all-reduce, s32[1024]{0:T(1024)S(1)} %iota_add_fusion, bf16[2048,3584]{1,0:T(8,128)(2,1)} %all-gather.2.cloned.1.call-done, bf16[1024,3584]{1,0:T(8,128)(2,1)} %param.5), kind=kOutput, calls=%fused_computation.1 | convolution fusion | flops 15047061504 | bytes 22048768 | tf_op jit(solution)/shard_map/dot_general | solution.py:14
  141.4 38.7 %all-reduce.1 = f32[2048]{0:T(1024)S(1)} all-reduce(f32[2048]{0:T(1024)S(1)} %get-tuple-element.2), channel_id=2, replica_groups=mesh['grp'=4,'vocab'=8] {'grp','vocab'}, use_global_device_ids=true, to_apply=%region_1.2.clone | all-reduce | flops 2048 | bytes 16384
  180.1 0.0 copy-done
  180.1 0.2 convolution_bitcast_fusion
  180.3 40.6 %all-reduce.3 = (f32[2048]{0:T(1024)S(1)}, f32[16]{0:T(128)}) all-reduce(f32[2048]{0:T(1024)S(1)} %get-tuple-element.3, f32[16]{0:T(128)S(1)} %convolution_bitcast_fusion), channel_id=3, replica_groups=mesh['grp'=4,'vocab'=8] {'grp','vocab'}, use_global_device_ids=true, to_apply=%region_3.4.clone | all-reduce | flops 2064 | bytes 16512
  220.9 0.6 fusion.1
  (2 shorter events, 0.0 us)
Async XLA Ops:
  7.2 112.2 %all-gather.2.cloned.1.call-start = ((), (), s32[]{:S(2)}) async-start(), calls=%async_computation | async-start | bytes 15138816 | tf_op jit(solution)/shard_map/all_gather | solution.py:31
  52.1 128.0 %copy-start = (s32[64]{0:T(128)S(1)}, s32[64]{0:T(128)}, u32[]{:S(2)}) copy-start(s32[64]{0:T(128)} %param.7) | copy-start | bytes 772
Sparse Core Ops, SparseCore 0:
  10.8 108.5 all-gather.1
where the time goes:
time: 229 us; the launch traced here: 228 us
  blocking collectives  123 us (54%)
  waiting for transfers between devices  68 us (30%)
  matrix products  22.2 us (10%)
  between operations  14.1 us (6%)
    unnamed x3, blocking collectives  123 us
    all_gather x1, waiting for transfers between devices, body(): lax.all_gather(hidden, ('grp', 'vocab'), axis=0, tiled=True)  67.3 us
    dot_general x1, matrix products, partial_stats(): lax.dot_general(rows_hidden, table, (((1,), (1,)), ((), ())), preferred_e...  22 us
  transfers between devices with their start and end apart: 1, of which 1 were waited for; matrix products, arithmetic and copies ran while one was open for 0% of the time, Pallas kernels for 0%

commit v1 on v0

v1 whole, which is shorter than its diff:
```python
import functools

import jax
import jax.numpy as jnp
from jax import lax
from jax.experimental import pallas as pl
from jax.experimental.pallas import tpu as pltpu
from jax.sharding import PartitionSpec as P

DOC_GRP = 4
LANES = 128
CORES = 2
MESH = pl.DeviceIdType.MESH

soft_cap = 30.0
zloss_coef = 0.0001


def kernel(dims, hid_ref, emb_ref, tgt_ref, seg_ref, loss_ref, doc_ref, buf, emb, tgs, sums, parts, docs,
           local_sem, send_sem, recv_sem, small_send, small_recv):
    NA, NB, Z, X, V, N, U, chunk = dims
    nb, rows, depth = buf.shape
    R = rows // U
    shard = emb.shape[0]
    n_docs = doc_ref.shape[1]
    g, v = lax.axis_index("grp"), lax.axis_index("vocab")
    me = g * V + v
    core, y, x, z = g % CORES, g // CORES, v % X, v // X
    swap = NA == NB

    def turn(c, p, q):
        return (jnp.where(c == 0, p, q), jnp.where(c == 0, q, p)) if swap else (p, q)

    a, b = turn(core, x, y)

    def device(c, aa, bb, zz):
        xx, yy = turn(c, aa, bb)
        return (yy * CORES + c, zz * X + xx)

    def pos(c, aa, bb, zz):
        return ((c * Z + zz) * NB + bb) * NA + aa

    def natural(c, aa, bb, zz):
        gg, vv = device(c, aa, bb, zz)
        return gg * V + vv

    def other(k):
        t = (me + k) % N
        return (t // V, t % V), t

    own = pos(core, a, b, z)
    load_hid = pltpu.make_async_copy(hid_ref, buf.at[own], local_sem.at[0])
    load_emb = pltpu.make_async_copy(emb_ref, emb, local_sem.at[1])
    load_tgt = pltpu.make_async_copy(tgt_ref, tgs.at[me], local_sem.at[2])
    load_hid.start()
    load_tgt.start()

    barrier = pltpu.get_barrier_semaphore()

    @pl.loop(1, N)
    def _(k):
        pl.semaphore_signal(barrier, inc=1, device_id=other(k)[0], device_id_type=MESH)

    load_emb.start()
    load_hid.wait()
    load_tgt.wait()
    pl.semaphore_wait(barrier, N - 1)

    def copy(p, u, d, dev):
        piece = buf.at[p, pl.ds(u * R, R)]
        return pltpu.make_async_remote_copy(
            piece, piece, send_sem.at[p * U + u, d], recv_sem.at[p * U + u], device_id=dev, device_id_type=MESH
        )

    def traverse(start):
        def put(p, u, d, at, size, dev):
            @pl.when((at >= 0) & (at < size))
            def _():
                c = copy(p, u, d, dev(at))
                c.start() if start else c.wait_send()

        def z_way(p, u, d, sgn):
            put(p, u, d, z + sgn, Z, lambda w: device(core, a, b, w))

        def a_way(p, u, d, sgn):
            put(p, u, d, a + sgn, NA, lambda w: device(core, w, b, z))

        def b_way(p, u, d, sgn):
            put(p, u, d, b + sgn, NB, lambda w: device(core, a, w, z))

        def twin(p, u):
            c = copy(p, u, 6, device_of_twin)
            c.start() if start else c.wait_send()

        def z_both(p, u):
            z_way(p, u, 0, 1)
            z_way(p, u, 1, -1)

        def a_both(p, u):
            a_way(p, u, 2, 1)
            a_way(p, u, 3, -1)

        def b_both(p, u):
            b_way(p, u, 4, 1)
            b_way(p, u, 5, -1)

        def arrive(p, u):
            if start:
                copy(p, u, 6, device_of_twin).wait_recv()

        if U > 1:
            a_both(own, 1)
        z_both(own, 0)
        b_both(own, 0)
        a_both(own, 0)
        if U > 1:
            z_both(own, 1)
            b_both(own, 1)
        for u in range(U):
            twin(own, u)

        def across_a(zz, u, extra):
            for da in range(1, NA):
                for sgn in (1, -1):
                    at = a + sgn * da

                    @pl.when((at >= 0) & (at < NA))
                    def _():
                        p = pos(core, at, b, zz)
                        arrive(p, u)
                        a_way(p, u, 2 if sgn < 0 else 3, -sgn)
                        if extra:
                            z_both(p, u)
                        b_both(p, u)
                        twin(p, u)

        def sides(s, fn):
            @pl.loop(0, 2)
            def _(side):
                zz = z + (1 - 2 * side) * s

                @pl.when((zz >= 0) & (zz < Z) & ((s > 0) | (side == 0)))
                def _():
                    fn(zz, side)

        if U > 1:
            across_a(z, 1, True)

        def z_arrivals(zz, side):
            onward = 2 * side - 1

            def one(p, u):
                arrive(p, u)
                put(p, u, 1 - side, z + onward, Z, lambda w: device(core, a, b, w))

            p = pos(core, a, b, zz)
            one(p, 0)
            a_both(p, 0)
            b_both(p, 0)
            twin(p, 0)
            for u in range(1, U):
                @pl.loop(0, NA)
                def _(k):
                    q = pos(core, (a + k) % NA, b, zz)
                    one(q, u)
                    b_both(q, u)
                    twin(q, u)

        def late(zz, side):
            across_a(zz, 0, False)

        def b_arrivals(zz, side):
            for u in range(U):
                @pl.loop(0, NA)
                def _(k):
                    for db in range(1, NB):
                        for sgn in (1, -1):
                            at = b + sgn * db

                            @pl.when((at >= 0) & (at < NB))
                            def _():
                                p = pos(core, (a + k) % NA, at, zz)
                                arrive(p, u)
                                b_way(p, u, 4 if sgn < 0 else 5, -sgn)
                                twin(p, u)

        @pl.loop(1, Z + 1)
        def _(s):
            @pl.when(s < Z)
            def _():
                sides(s, z_arrivals)

            sides(s - 1, late)
            sides(s - 1, b_arrivals)
            if start:
                @pl.when(s == 1)
                def _():
                    load_emb.wait()
                    few = tgs.at[pl.ds(0, N - 1)]
                    pltpu.make_async_remote_copy(
                        few, few, small_send.at[0], small_recv.at[0], device_id=device_of_twin, device_id_type=MESH
                    ).wait()

                sides(s - 1, batch)

    device_of_twin = ((g // CORES) * CORES + 1 - core, v)

    @pl.loop(1, N)
    def _(k):
        pltpu.make_async_remote_copy(
            tgs.at[me], tgs.at[me], small_send.at[0], small_recv.at[0], device_id=other(k)[0], device_id_type=MESH
        ).start()

    blocks = NA * NB
    first_id = (v * lax.axis_size("grp") + g) * shard

    def batch(zz, side):
        @pl.loop(0, CORES)
        def _(k):
            c = (core + k) % CORES
            base = pos(c, 0, 0, zz)

            @pl.when(k == 1)
            def _():
                @pl.loop(0, blocks * U)
                def _(i):
                    copy(base + i // U, i % U, 6, device_of_twin).wait_recv()

            where_to = [natural(c, i % NA, i // NA, zz) for i in range(blocks)]
            wanted = jnp.concatenate([tgs[w] for w in where_to], axis=1)
            tokens = blocks * rows

            def step(i, carry):
                start = pl.multiple_of(i * chunk, chunk)
                logits = lax.dot_general(
                    emb[pl.ds(start, chunk), :],
                    buf[pl.ds(base, blocks)].reshape(tokens, depth),
                    (((1,), (1,)), ((), ())),
                    preferred_element_type=jnp.float32,
                )
                capped = soft_cap * jnp.tanh(logits * (1.0 / soft_cap))
                ids = lax.broadcasted_iota(jnp.int32, (chunk, tokens), 0)
                hit = ids == (wanted - (first_id + start))
                return (
                    carry[0] + jnp.sum(jnp.exp(capped - soft_cap), axis=0, keepdims=True),
                    carry[1] + jnp.sum(jnp.where(hit, capped, 0.0), axis=0, keepdims=True),
                )

            zero = jnp.zeros((1, tokens), jnp.float32)
            total, picked = lax.fori_loop(0, shard // chunk, step, (zero, zero))
            for i, w in enumerate(where_to):
                sums[w, 0:1, :] = total[:, i * rows : (i + 1) * rows]
                sums[w, 1:2, :] = picked[:, i * rows : (i + 1) * rows]

    traverse(True)

    def exchange(source_of, dest, which):
        @pl.loop(1, N)
        def _(k):
            dev, t = other(k)
            pltpu.make_async_remote_copy(
                source_of(t), dest.at[me], small_send.at[which], small_recv.at[which], device_id=dev, device_id_type=MESH
            ).start()

    def settle(dest, which):
        few = dest.at[pl.ds(0, N - 1)]
        pltpu.make_async_remote_copy(
            few, few, small_send.at[which], small_recv.at[which], device_id=device_of_twin, device_id_type=MESH
        ).wait()

    exchange(lambda t: sums.at[t], parts, 1)
    parts[me] = sums[me]
    traverse(False)
    settle(parts, 1)

    both = jnp.sum(parts[...], axis=0)
    lse = soft_cap + jnp.log(both[0:1, :])
    zterm = zloss_coef * lse * lse
    loss_ref[...] = lse - both[1:2, :] + zterm
    width = docs.shape[2]
    of_doc = lax.broadcasted_iota(jnp.int32, (n_docs, rows), 0) == seg_ref[...]
    column = jnp.sum(jnp.where(of_doc, zterm, 0.0), axis=1, keepdims=True)
    diagonal = lax.broadcasted_iota(jnp.int32, (n_docs, width), 0) == lax.broadcasted_iota(
        jnp.int32, (n_docs, width), 1
    )
    docs[me] = jnp.sum(jnp.where(diagonal, column, 0.0), axis=0, keepdims=True)
    exchange(lambda t: docs.at[me], docs, 2)
    settle(docs, 2)
    doc_ref[...] = jnp.sum(docs[...], axis=0)[:, :n_docs]


def solution(mesh):
    G, V = mesh.shape["grp"], mesh.shape["vocab"]
    N = G * V
    Y = G // CORES
    X = Y if V % Y == 0 else 1
    Z = V // X
    n_docs = DOC_GRP * G

    def body(hidden, embedding, targets, segments):
        rows, depth = hidden.shape
        shard = embedding.shape[0]
        U = 2 if rows % 32 == 0 else 1
        chunk = min(512, shard)
        dims = (X, Y, Z, X, V, N, U, chunk)
        width = -(-n_docs // LANES) * LANES
        any_spec = pl.BlockSpec(memory_space=pl.ANY)
        vmem = pl.BlockSpec(memory_space=pltpu.VMEM)
        loss, doc = pl.pallas_call(
            functools.partial(kernel, dims),
            out_shape=(
                jax.ShapeDtypeStruct((1, rows), jnp.float32),
                jax.ShapeDtypeStruct((1, n_docs), jnp.float32),
            ),
            in_specs=[any_spec, any_spec, vmem, vmem],
            out_specs=(vmem, vmem),
            scratch_shapes=[
                pltpu.VMEM((N, rows, depth), jnp.bfloat16),
                pltpu.VMEM((shard, depth), jnp.bfloat16),
                pltpu.VMEM((N, 1, rows), jnp.int32),
                pltpu.VMEM((N, 2, rows), jnp.float32),
                pltpu.VMEM((N, 2, rows), jnp.float32),
                pltpu.VMEM((N, 1, width), jnp.float32),
                pltpu.SemaphoreType.DMA((3,)),
                pltpu.SemaphoreType.DMA((N * U, 7)),
                pltpu.SemaphoreType.DMA((N * U,)),
                pltpu.SemaphoreType.DMA((3,)),
                pltpu.SemaphoreType.DMA((3,)),
            ],
            compiler_params=pltpu.CompilerParams(
                collective_id=0, has_side_effects=True, vmem_limit_bytes=60 * 1024 * 1024
            ),
        )(hidden, embedding, targets.reshape(1, rows), segments.reshape(1, rows))
        return (loss.reshape(rows), doc.reshape(n_docs))

    return jax.shard_map(
        body,
        mesh=mesh,
        in_specs=(
            P(("grp", "vocab"), None),
            P(("vocab", "grp"), None),
            P(("grp", "vocab")),
            P(("grp", "vocab")),
        ),
        out_specs=(P(("grp", "vocab")), P()),
        check_vma=False,
    )
```

time: 229 us -> 107 us (0.47)
  blocking collectives: 123 us -> 0 us
  Pallas kernels: 0 us -> 104 us
  waiting for transfers between devices: 68 us -> 0 us
  matrix products: 22.2 us -> 0 us
  between operations: 14.1 us -> 0.64 us
    unnamed x3 -> x0, blocking collectives: 123 us -> none
    pallas_call x0 -> x1, Pallas kernels: none -> 104 us  [body(): pl.pallas_call(functools.partial(kernel, dims), out_shape=(jax.ShapeDtype...]
    all_gather x1 -> x0, waiting for transfers between devices: 67.3 us -> none  [body(): lax.all_gather(hidden, ('grp', 'vocab'), axis=0, tiled=True)]
    dot_general x2 -> x0, matrix products: 22.2 us -> none  [the longest x1 22 us: partial_stats(): lax.dot_general(rows_hidden, table, (((1,), (1,)), ((), ())), preferred_e...]
  transfers between devices with their start and end apart: 1 -> 0, of which waited for: 1 -> 0; matrix products, arithmetic and copies ran while one was open for 0% -> 0% of each run, Pallas kernels for 0% -> 0%
where the time goes in v1:
time: 107 us
  Pallas kernels  104 us (97%)
  local copies, waits for them, and re-layouts  2.25 us (2%)
    pallas_call x1, Pallas kernels, body(): pl.pallas_call(functools.partial(kernel, dims), out_shape=(jax.ShapeDtype...  104 us
    unnamed x2, local copies, waits for them, and re-layouts  2.25 us

profile of v1, /device:TPU:0, one launch (start us, length us, event | category | flops | bytes accessed | tf_op | source)
XLA Modules:
  0.0 106.6 jit_solution(13327823507099997413)
XLA Ops:
  0.6 103.7 %shard_map.59 = (f32[1,64]{1,0:T(1,128)}, f32[1,16]{1,0:T(1,128)}) custom-call(bf16[64,3584]{1,0:T(8,128)(2,1)} %hid_ref.1, bf16[1024,3584]{1,0:T(8,128)(2,1)} %emb_ref.1, s32[1,64]{1,0:T(1,128)} %bitcast.4, s32[1,64]{1,0:T(1,128)} %bitcast.5), custom_call_target="tpu_custom_call" | custom-call | tf_op jit(solution)/shard_map/pallas_call | solution.py:309
  104.3 1.1 %copy.8 = f32[64]{0:T(128)} copy(f32[64]{0:T(128)} %bitcast.7) | data formatting | bytes 512
  105.4 1.1 %copy.9 = f32[16]{0:T(128)} copy(f32[16]{0:T(128)} %bitcast.6) | data formatting | bytes 128

commit v2 on v1

--- a/solution.py
+++ b/solution.py
@@ -96,42 +96,55 @@
             z_way(p, u, 0, 1)
             z_way(p, u, 1, -1)
 
-        def a_both(p, u):
-            a_way(p, u, 2, 1)
-            a_way(p, u, 3, -1)
-
-        def b_both(p, u):
-            b_way(p, u, 4, 1)
-            b_way(p, u, 5, -1)
+        def mid_way(p, u, sgn):
+            (a_way if u == 0 else b_way)(p, u, 2 if sgn > 0 else 3, sgn)
+
+        def last_way(p, u, sgn):
+            (b_way if u == 0 else a_way)(p, u, 4 if sgn > 0 else 5, sgn)
+
+        def mid_both(p, u):
+            mid_way(p, u, 1)
+            mid_way(p, u, -1)
+
+        def last_both(p, u):
+            last_way(p, u, 1)
+            last_way(p, u, -1)
+
+        def role(u):
+            return (a, NA, b, NB) if u == 0 else (b, NB, a, NA)
+
+        def at_role(u, mid, last, zz):
+            return pos(core, mid, last, zz) if u == 0 else pos(core, last, mid, zz)
 
         def arrive(p, u):
             if start:
                 copy(p, u, 6, device_of_twin).wait_recv()
 
         if U > 1:
-            a_both(own, 1)
+            mid_both(own, 1)
         z_both(own, 0)
-        b_both(own, 0)
-        a_both(own, 0)
+        last_both(own, 0)
+        mid_both(own, 0)
         if U > 1:
             z_both(own, 1)
-            b_both(own, 1)
+            last_both(own, 1)
         for u in range(U):
             twin(own, u)
 
-        def across_a(zz, u, extra):
-            for da in range(1, NA):
+        def across_mid(zz, u, extra):
+            here, size, last, _ = role(u)
+            for step in range(1, size):
                 for sgn in (1, -1):
-                    at = a + sgn * da
-
-                    @pl.when((at >= 0) & (at < NA))
+                    at = here + sgn * step
+
+                    @pl.when((at >= 0) & (at < size))
                     def _():
-                        p = pos(core, at, b, zz)
+                        p = at_role(u, at, last, zz)
                         arrive(p, u)
-                        a_way(p, u, 2 if sgn < 0 else 3, -sgn)
+                        mid_way(p, u, -sgn)
                         if extra:
                             z_both(p, u)
-                        b_both(p, u)
+                        last_both(p, u)
                         twin(p, u)
 
         def sides(s, fn):
@@ -144,64 +157,73 @@
                     fn(zz, side)
 
         if U > 1:
-            across_a(z, 1, True)
-
-        def z_arrivals(zz, side):
-            onward = 2 * side - 1
-
-            def one(p, u):
-                arrive(p, u)
-                put(p, u, 1 - side, z + onward, Z, lambda w: device(core, a, b, w))
-
+            across_mid(z, 1, True)
+
+        def from_z(p, u, side):
+            arrive(p, u)
+            put(p, u, 1 - side, z + 2 * side - 1, Z, lambda w: device(core, a, b, w))
+
+        def z_first(zz, side):
             p = pos(core, a, b, zz)
-            one(p, 0)
-            a_both(p, 0)
-            b_both(p, 0)
+            from_z(p, 0, side)
+            mid_both(p, 0)
+            last_both(p, 0)
             twin(p, 0)
-            for u in range(1, U):
-                @pl.loop(0, NA)
-                def _(k):
-                    q = pos(core, (a + k) % NA, b, zz)
-                    one(q, u)
-                    b_both(q, u)
-                    twin(q, u)
+
+        def z_second(zz, side, k, u):
+            here, size, last, _ = role(u)
+            q = at_role(u, (here + k) % size, last, zz)
+            from_z(q, u, side)
+            last_both(q, u)
+            twin(q, u)
 
         def late(zz, side):
-            across_a(zz, 0, False)
+            across_mid(zz, 0, False)
 
         def b_arrivals(zz, side):
             for u in range(U):
-                @pl.loop(0, NA)
+                here, size, last, length = role(u)
+
+                @pl.loop(0, size)
                 def _(k):
-                    for db in range(1, NB):
+                    for step in range(1, length):
                         for sgn in (1, -1):
-                            at = b + sgn * db
-
-                            @pl.when((at >= 0) & (at < NB))
+                            at = last + sgn * step
+
+                            @pl.when((at >= 0) & (at < length))
                             def _():
-                                p = pos(core, (a + k) % NA, at, zz)
+                                p = at_role(u, (here + k) % size, at, zz)
                                 arrive(p, u)
-                                b_way(p, u, 4 if sgn < 0 else 5, -sgn)
+                                last_way(p, u, -sgn)
                                 twin(p, u)
 
-        @pl.loop(1, Z + 1)
+        @pl.loop(1, Z + 2)
         def _(s):
             @pl.when(s < Z)
             def _():
-                sides(s, z_arrivals)
-
-            sides(s - 1, late)
-            sides(s - 1, b_arrivals)
-            if start:
-                @pl.when(s == 1)
-                def _():
-                    load_emb.wait()
-                    few = tgs.at[pl.ds(0, N - 1)]
-                    pltpu.make_async_remote_copy(
-                        few, few, small_send.at[0], small_recv.at[0], device_id=device_of_twin, device_id_type=MESH
-                    ).wait()
-
-                sides(s - 1, batch)
+                sides(s, z_first)
+                for u in range(1, U):
+                    @pl.loop(0, role(u)[1])
+                    def _(k):
+                        sides(s, lambda zz, side: z_second(zz, side, k, u))
+
+            @pl.when(s <= Z)
+            def _():
+                sides(s - 1, late)
+
+            @pl.when(s >= 2)
+            def _():
+                sides(s - 2, b_arrivals)
+                if start:
+                    @pl.when(s == 2)
+                    def _():
+                        load_emb.wait()
+                        few = tgs.at[pl.ds(0, N - 1)]
+                        pltpu.make_async_remote_copy(
+                            few, few, small_send.at[0], small_recv.at[0], device_id=device_of_twin, device_id_type=MESH
+                        ).wait()
+
+                    sides(s - 2, batch)
 
     device_of_twin = ((g // CORES) * CORES + 1 - core, v)
 
@@ -251,6 +273,13 @@
             for i, w in enumerate(where_to):
                 sums[w, 0:1, :] = total[:, i * rows : (i + 1) * rows]
                 sums[w, 1:2, :] = picked[:, i * rows : (i + 1) * rows]
+            for w in where_to:
+                @pl.when(w != me)
+                def _():
+                    pltpu.make_async_remote_copy(
+                        sums.at[w], parts.at[me], small_send.at[1], small_recv.at[1],
+                        device_id=(w // V, w % V), device_id_type=MESH,
+                    ).start()
 
     traverse(True)
 
@@ -268,7 +297,6 @@
             few, few, small_send.at[which], small_recv.at[which], device_id=device_of_twin, device_id_type=MESH
         ).wait()
 
-    exchange(lambda t: sums.at[t], parts, 1)
     parts[me] = sums[me]
     traverse(False)
     settle(parts, 1)
@@ -301,7 +329,7 @@
         rows, depth = hidden.shape
         shard = embedding.shape[0]
         U = 2 if rows % 32 == 0 else 1
-        chunk = min(512, shard)
+        chunk = min(1024, shard)
         dims = (X, Y, Z, X, V, N, U, chunk)
         width = -(-n_docs // LANES) * LANES
         any_spec = pl.BlockSpec(memory_space=pl.ANY)

time: 107 us -> 86.7 us (0.81)
  Pallas kernels: 104 us -> 83.6 us
    pallas_call x1, Pallas kernels: 104 us -> 83.6 us  [body(): pl.pallas_call(functools.partial(kernel, dims), out_shape=(jax.ShapeDtype...]
where the time goes in v2:
time: 86.7 us; the launch traced here: 86.5 us
  Pallas kernels  83.6 us (96%)
  local copies, waits for them, and re-layouts  2.25 us (3%)
    pallas_call x1, Pallas kernels, body(): pl.pallas_call(functools.partial(kernel, dims), out_shape=(jax.ShapeDtype...  83.6 us
    unnamed x2, local copies, waits for them, and re-layouts  2.25 us

profile of v2, /device:TPU:0, one launch (start us, length us, event | category | flops | bytes accessed | tf_op | source)
XLA Modules:
  0.0 86.5 jit_solution(14798909544732557334)
XLA Ops:
  0.6 83.6 %shard_map.59 = (f32[1,64]{1,0:T(1,128)}, f32[1,16]{1,0:T(1,128)}) custom-call(bf16[64,3584]{1,0:T(8,128)(2,1)} %hid_ref.1, bf16[1024,3584]{1,0:T(8,128)(2,1)} %emb_ref.1, s32[1,64]{1,0:T(1,128)} %bitcast.4, s32[1,64]{1,0:T(1,128)} %bitcast.5), custom_call_target="tpu_custom_call" | custom-call | tf_op jit(solution)/shard_map/pallas_call | solution.py:337
  84.2 1.1 %copy.8 = f32[64]{0:T(128)} copy(f32[64]{0:T(128)} %bitcast.7) | data formatting | bytes 512
  85.3 1.1 %copy.9 = f32[16]{0:T(128)} copy(f32[16]{0:T(128)} %bitcast.6) | data formatting | bytes 128

commit v3 on v2

--- a/solution.py
+++ b/solution.py
@@ -72,6 +72,13 @@
             piece, piece, send_sem.at[p * U + u, d], recv_sem.at[p * U + u], device_id=dev, device_id_type=MESH
         )
 
+    def send_targets():
+        @pl.loop(1, N)
+        def _(k):
+            pltpu.make_async_remote_copy(
+                tgs.at[me], tgs.at[me], small_send.at[0], small_recv.at[0], device_id=other(k)[0], device_id_type=MESH
+            ).start()
+
     def traverse(start):
         def put(p, u, d, at, size, dev):
             @pl.when((at >= 0) & (at < size))
@@ -128,6 +135,8 @@
         if U > 1:
             z_both(own, 1)
             last_both(own, 1)
+        if start:
+            send_targets()
         for u in range(U):
             twin(own, u)
 
@@ -226,12 +235,6 @@
                     sides(s - 2, batch)
 
     device_of_twin = ((g // CORES) * CORES + 1 - core, v)
-
-    @pl.loop(1, N)
-    def _(k):
-        pltpu.make_async_remote_copy(
-            tgs.at[me], tgs.at[me], small_send.at[0], small_recv.at[0], device_id=other(k)[0], device_id_type=MESH
-        ).start()
 
     blocks = NA * NB
     first_id = (v * lax.axis_size("grp") + g) * shard
@@ -298,7 +301,6 @@
         ).wait()
 
     parts[me] = sums[me]
-    traverse(False)
     settle(parts, 1)
 
     both = jnp.sum(parts[...], axis=0)
@@ -313,6 +315,7 @@
     )
     docs[me] = jnp.sum(jnp.where(diagonal, column, 0.0), axis=0, keepdims=True)
     exchange(lambda t: docs.at[me], docs, 2)
+    traverse(False)
     settle(docs, 2)
     doc_ref[...] = jnp.sum(docs[...], axis=0)[:, :n_docs]
 

time: 86.7 us -> 86.4 us (level)
  no operation moved by 1% of the time
where the time goes in v3:
time: 86.4 us; the launch traced here: 86.2 us
  Pallas kernels  83.3 us (96%)
  local copies, waits for them, and re-layouts  2.25 us (3%)
    pallas_call x1, Pallas kernels, body(): pl.pallas_call(functools.partial(kernel, dims), out_shape=(jax.ShapeDtype...  83.3 us
    unnamed x2, local copies, waits for them, and re-layouts  2.25 us

profile of v3, /device:TPU:0, one launch (start us, length us, event | category | flops | bytes accessed | tf_op | source)
XLA Modules:
  0.0 86.2 jit_solution(4184970693049576522)
XLA Ops:
  0.6 83.3 %shard_map.59 = (f32[1,64]{1,0:T(1,128)}, f32[1,16]{1,0:T(1,128)}) custom-call(bf16[64,3584]{1,0:T(8,128)(2,1)} %hid_ref.1, bf16[1024,3584]{1,0:T(8,128)(2,1)} %emb_ref.1, s32[1,64]{1,0:T(1,128)} %bitcast.4, s32[1,64]{1,0:T(1,128)} %bitcast.5), custom_call_target="tpu_custom_call" | custom-call | tf_op jit(solution)/shard_map/pallas_call | solution.py:340
  83.9 1.1 %copy.8 = f32[64]{0:T(128)} copy(f32[64]{0:T(128)} %bitcast.7) | data formatting | bytes 512
  85.0 1.1 %copy.9 = f32[16]{0:T(128)} copy(f32[16]{0:T(128)} %bitcast.6) | data formatting | bytes 128
